TPU v7x, 8 devices: a whole 2x2x1 slice. The times are simulated.
8 devices in a mesh: dp: 1 (over z), cz: 2 (over y), cy: 2 (over x), cx: 2 (over core).
Axes of the slice: x: 2, y: 2, z: 1, core: 2. Of those that a mesh axis runs over, the one named last changes fastest.
Arguments:
- x_act: bfloat16 [8192, 3072], P(('dp', 'cx', 'cz'), 'cy')
- w_up: bfloat16 [3072, 8192], P('cy', ('cz', 'cx'))
- w_down: bfloat16 [8192, 3072], P('cz', ('cy', 'cx'))
- z_grad: bfloat16 [8192, 3072], P(('dp', 'cx', 'cz'), 'cy')
Outputs:
- output 1: bfloat16 [8192, 3072], P(('dp', 'cx', 'cz'), 'cy')
- output 2: bfloat16 [3072, 8192], P(('dp', 'cy'), ('cz', 'cx'))
- output 3: bfloat16 [8192, 3072], P(('dp', 'cz'), ('cy', 'cx'))
All inputs are finite; a program needn't handle non-finite values.
Results may differ from a plain program's by a relative error of at most 0.0114789.
Values are sent between devices in bfloat16 or wider.
A program may use at most 1 GiB of HBM per device.

v0:
```python
import math
import jax
import jax.numpy as jnp
from jax import lax
from jax.sharding import PartitionSpec as P

GELU_COEF = 0.044715
SQRT_TWO_PI = math.sqrt(2.0 / math.pi)
CONTRACT_LAST = (((1,), (1,)), ((), ()))
CONTRACT_FIRST = (((0,), (0,)), ((), ()))


def gelu_parts(pre_act):
    inner_arg = SQRT_TWO_PI * (pre_act + GELU_COEF * pre_act * pre_act * pre_act)
    tanh_val = jnp.tanh(inner_arg)
    gelu_val = 0.5 * pre_act * (1.0 + tanh_val)
    gelu_slope = 0.5 * (1.0 + tanh_val) + 0.5 * pre_act * (1.0 - tanh_val * tanh_val) * SQRT_TWO_PI * (1.0 + 3.0 * GELU_COEF * pre_act * pre_act)
    return gelu_val, gelu_slope


def solution(mesh):
    row_spec = P(("dp", "cx", "cz"), "cy")
    up_spec = P("cy", ("cz", "cx"))
    down_spec = P("cz", ("cy", "cx"))
    up_out = P(("dp", "cy"), ("cz", "cx"))
    down_out = P(("dp", "cz"), ("cy", "cx"))

    def local_step(x_act, w_up, w_down, z_grad):
        x_full = lax.all_gather(x_act, "cz", axis=0, tiled=True)
        up_full = lax.all_gather(w_up, "cx", axis=1, tiled=True)
        pre_part = jnp.dot(x_full, up_full, preferred_element_type=jnp.float32)
        pre_sum = lax.psum_scatter(pre_part, "cy", scatter_dimension=0, tiled=True)
        pre_act = pre_sum.astype(jnp.bfloat16).astype(jnp.float32)
        gelu_val, gelu_slope = gelu_parts(pre_act)
        hidden = gelu_val.astype(jnp.bfloat16)
        z_full = lax.all_gather(z_grad, "cz", axis=0, tiled=True)
        down_full = lax.all_gather(w_down, "cx", axis=1, tiled=True)
        h_part = lax.dot_general(z_full, down_full, CONTRACT_LAST, preferred_element_type=jnp.float32)
        h_grad = lax.psum_scatter(h_part, "cy", scatter_dimension=0, tiled=True)
        pre_grad = (h_grad * gelu_slope).astype(jnp.bfloat16)
        hidden_full = lax.all_gather(hidden, "cy", axis=0, tiled=True)
        down_part = lax.dot_general(hidden_full, z_full, CONTRACT_FIRST, preferred_element_type=jnp.float32)
        down_grad = lax.psum_scatter(down_part, "cx", scatter_dimension=1, tiled=True).astype(jnp.bfloat16)
        grad_full = lax.all_gather(pre_grad, "cy", axis=0, tiled=True)
        x_part = lax.dot_general(grad_full, up_full, CONTRACT_LAST, preferred_element_type=jnp.float32)
        x_grad = lax.psum_scatter(x_part, "cz", scatter_dimension=0, tiled=True).astype(jnp.bfloat16)
        up_part = lax.dot_general(x_full, grad_full, CONTRACT_FIRST, preferred_element_type=jnp.float32)
        up_grad = lax.psum_scatter(up_part, "cx", scatter_dimension=1, tiled=True).astype(jnp.bfloat16)
        return (x_grad, up_grad, down_grad)

    return jax.shard_map(local_step, mesh=mesh, in_specs=(row_spec, up_spec, down_spec, row_spec), out_specs=(row_spec, up_out, down_out), check_vma=False)
```

profile of v0, /device:TPU:0, one launch (start us, length us, event | category | flops | bytes accessed | tf_op | source)
XLA Modules:
  0.0 3051.0 jit_solution(15292289020041511979)
XLA Ops:
  7.2 0.0 all-gather.9.cloned.1.call-start
  7.2 0.7 all-gather.9.cloned.1.call-update
  7.9 0.0 all-gather.7.cloned.1.call-start
  7.9 0.7 all-gather.7.cloned.1.call-update
  8.6 0.0 all-gather.11.cloned.1.call-start
  8.7 0.7 all-gather.11.cloned.1.call-update
  9.4 0.0 all-gather.13.cloned.1.call-start
  9.4 0.5 all-gather.13.cloned.1.call-update
  10.0 0.0 reduce-scatter.6.cloned.1.call-start
  10.0 25.2 all-gather.9.cloned.1.call-done
  35.2 153.3 %all-gather.7.cloned.1.call-done = bf16[4096,1536]{1,0:T(8,128)(2,1)} async-done(((bf16[2048,1536]{1,0:T(8,128)(2,1)}), bf16[4096,1536]{1,0:T(8,128)(2,1)}) %all-gather.7.cloned.1.call-update) | async-done | bytes 12582928 | tf_op jit(solution)/shard_map/all_gather | solution.py:36
  188.5 61.9 %fusion.11 = f32[4096,4096]{1,0:T(8,128)} fusion(bf16[4096,1536]{1,0:T(8,128)(2,1)} %all-gather.7.cloned.1.call-done, bf16[4096,1536]{1,0:T(8,128)(2,1)} %all-gather.9.cloned.1.call-done), kind=kOutput, calls=%fused_computation.19 | convolution fusion | flops 51539607552 | bytes 92274688 | tf_op jit(solution)/shard_map/dot_general | solution.py:38
  250.4 0.0 reduce-scatter.6.cloned.1.call-update
  250.4 0.5 reduce-scatter.8.cloned.1.call-start
  251.0 89.7 %all-gather.11.cloned.1.call-done = bf16[4096,1536]{1,0:T(8,128)(2,1)} async-done(((bf16[2048,1536]{1,0:T(8,128)(2,1)}), bf16[4096,1536]{1,0:T(8,128)(2,1)}) %all-gather.11.cloned.1.call-update) | async-done | bytes 12582928 | tf_op jit(solution)/shard_map/all_gather | solution.py:29
  340.6 24.3 all-gather.13.cloned.1.call-done
  364.9 61.7 %fusion.12 = f32[4096,4096]{1,0:T(8,128)} fusion(bf16[4096,1536]{1,0:T(8,128)(2,1)} %all-gather.11.cloned.1.call-done, bf16[1536,4096]{1,0:T(8,128)(2,1)} %all-gather.13.cloned.1.call-done), kind=kOutput, calls=%fused_computation.20 | convolution fusion | flops 51539607552 | bytes 92274688 | tf_op jit(solution)/shard_map/dot_general | solution.py:31
  426.6 0.0 reduce-scatter.8.cloned.1.call-update
  426.6 0.0 all-gather.15.cloned.1.call-start
  426.6 667.2 %reduce-scatter.6.cloned.1.call-done = f32[2048,4096]{1,0:T(8,128)} async-done(((f32[4096,4096]{1,0:T(8,128)}), f32[2048,4096]{1,0:T(8,128)}) %reduce-scatter.6.cloned.1.call-update) | async-done | bytes 33554448 | tf_op jit(solution)/shard_map/reduce_scatter | solution.py:39
  1093.9 727.8 %reduce-scatter.8.cloned.1.call-done = f32[2048,4096]{1,0:T(8,128)} async-done(((f32[4096,4096]{1,0:T(8,128)}), f32[2048,4096]{1,0:T(8,128)}) %reduce-scatter.8.cloned.1.call-update) | async-done | bytes 33554448 | tf_op jit(solution)/shard_map/reduce_scatter | solution.py:32
  1821.6 39.3 %fusion.7 = (bf16[2048,4096]{1,0:T(8,128)(2,1)}, bf16[2048,4096]{1,0:T(8,128)(2,1)}) fusion(f32[2048,4096]{1,0:T(8,128)} %reduce-scatter.8.cloned.1.call-done, f32[2048,4096]{1,0:T(8,128)} %reduce-scatter.6.cloned.1.call-done), kind=kLoop, calls=%fused_computation.14 | loop fusion | flops 192937984 | bytes 100663296 | tf_op jit(solution)/shard_map/convert_element_type | solution.py:35
  1860.9 0.0 all-gather.15.cloned.1.call-update
  1860.9 0.0 all-gather.17.cloned.1.call-start
  1861.0 0.7 all-gather.17.cloned.1.call-update
  1861.7 0.0 reduce-scatter.12.cloned.1.call-start
  1861.7 384.9 %all-gather.15.cloned.1.call-done = bf16[4096,4096]{1,0:T(8,128)(2,1)} async-done(((bf16[2048,4096]{1,0:T(8,128)(2,1)}), bf16[4096,4096]{1,0:T(8,128)(2,1)}) %all-gather.15.cloned.1.call-update) | async-done | bytes 33554448 | tf_op jit(solution)/shard_map/all_gather | solution.py:44
  2246.6 63.0 %convolution_bitcast_fusion = f32[1536,4096]{0,1:T(8,128)} fusion(bf16[4096,4096]{1,0:T(8,128)(2,1)} %all-gather.15.cloned.1.call-done, bf16[4096,1536]{1,0:T(8,128)(2,1)} %all-gather.11.cloned.1.call-done), kind=kOutput, calls=%fused_computation.18 | convolution fusion | flops 51539607552 | bytes 71303168 | tf_op jit(solution)/shard_map/dot_general | solution.py:47
  2309.6 0.0 reduce-scatter.12.cloned.1.call-update
  2309.6 0.0 reduce-scatter.14.cloned.1.call-start
  2309.7 324.0 %all-gather.17.cloned.1.call-done = bf16[4096,4096]{1,0:T(8,128)(2,1)} async-done(((bf16[2048,4096]{1,0:T(8,128)(2,1)}), bf16[4096,4096]{1,0:T(8,128)(2,1)}) %all-gather.17.cloned.1.call-update) | async-done | bytes 33554448 | tf_op jit(solution)/shard_map/all_gather | solution.py:41
  2633.6 63.2 %fusion.14 = f32[4096,1536]{1,0:T(8,128)} fusion(bf16[4096,4096]{1,0:T(8,128)(2,1)} %all-gather.17.cloned.1.call-done, bf16[4096,1536]{1,0:T(8,128)(2,1)} %all-gather.7.cloned.1.call-done), kind=kOutput, calls=%fused_computation.22 | convolution fusion | flops 51539607552 | bytes 71303168 | tf_op jit(solution)/shard_map/dot_general | solution.py:42
  2696.9 0.0 reduce-scatter.14.cloned.1.call-update
  2696.9 0.0 reduce-scatter.10.cloned.1.call-start
  2697.0 62.3 %fusion.13 = f32[4096,1536]{1,0:T(8,128)} fusion(bf16[4096,4096]{1,0:T(8,128)(2,1)} %all-gather.15.cloned.1.call-done, bf16[1536,4096]{1,0:T(8,128)(2,1)} %all-gather.13.cloned.1.call-done), kind=kOutput, calls=%fused_computation.21 | convolution fusion | flops 51539607552 | bytes 71303168 | tf_op jit(solution)/shard_map/dot_general | solution.py:45
  2759.3 0.0 reduce-scatter.10.cloned.1.call-update
  2759.3 0.0 reduce-scatter.12.cloned.1.call-done
  2759.4 8.1 convert_element_type.25
  2767.4 8.6 copy.7
  2776.0 0.0 reduce-scatter.14.cloned.1.call-done
  2776.0 7.9 convert_element_type.27
  2783.9 252.1 %reduce-scatter.10.cloned.1.call-done = f32[2048,1536]{1,0:T(8,128)} async-done(((f32[4096,1536]{1,0:T(8,128)}), f32[2048,1536]{1,0:T(8,128)}) %reduce-scatter.10.cloned.1.call-update) | async-done | bytes 12582928 | tf_op jit(solution)/shard_map/reduce_scatter | solution.py:46
  3036.0 8.1 convert_element_type.24
Async XLA Ops:
  7.2 28.1 all-gather.9.cloned.1.call-start
  7.9 180.6 %all-gather.7.cloned.1.call-start = ((), (), s32[]{:S(2)}) async-start(), calls=%async_computation.5 | async-start | bytes 18874368 | tf_op jit(solution)/shard_map/all_gather | solution.py:36
  8.6 332.0 %all-gather.11.cloned.1.call-start = ((), (), s32[]{:S(2)}) async-start(), calls=%async_computation.8 | async-start | bytes 18874368 | tf_op jit(solution)/shard_map/all_gather | solution.py:29
  9.4 355.5 %all-gather.13.cloned.1.call-start = ((), (), s32[]{:S(2)}) async-start(), calls=%async_computation.9 | async-start | bytes 18874368 | tf_op jit(solution)/shard_map/all_gather | solution.py:30
  10.0 1083.9 %reduce-scatter.6.cloned.1.call-start = ((), (), s32[]{:S(2)}) async-start(), calls=%async_computation.7 | async-start | bytes 100663296 | tf_op jit(solution)/shard_map/reduce_scatter | solution.py:39
  250.4 1571.2 %reduce-scatter.8.cloned.1.call-start = ((), (), s32[]{:S(2)}) async-start(), calls=%async_computation.10 | async-start | bytes 100663296 | tf_op jit(solution)/shard_map/reduce_scatter | solution.py:32
  426.6 1820.0 %all-gather.15.cloned.1.call-start = ((), (), s32[]{:S(2)}) async-start(), calls=%async_computation.11 | async-start | bytes 50331648 | tf_op jit(solution)/shard_map/all_gather | solution.py:44
  1860.9 772.7 %all-gather.17.cloned.1.call-start = ((), (), s32[]{:S(2)}) async-start(), calls=%async_computation.14 | async-start | bytes 50331648 | tf_op jit(solution)/shard_map/all_gather | solution.py:41
  1861.7 897.7 %reduce-scatter.12.cloned.1.call-start = ((), (), s32[]{:S(2)}) async-start(), calls=%async_computation.13 | async-start | bytes 37748736 | tf_op jit(solution)/shard_map/reduce_scatter | solution.py:48
  2309.6 466.4 %reduce-scatter.14.cloned.1.call-start = ((), (), s32[]{:S(2)}) async-start(), calls=%async_computation.15 | async-start | bytes 37748736 | tf_op jit(solution)/shard_map/reduce_scatter | solution.py:43
  2696.9 339.1 %reduce-scatter.10.cloned.1.call-start = ((), (), s32[]{:S(2)}) async-start(), calls=%async_computation.12 | async-start | bytes 37748736 | tf_op jit(solution)/shard_map/reduce_scatter | solution.py:46
Sparse Core Ops, SparseCore 0:
  9.5 25.6 all-gather.8
  36.7 151.7 all-gather.6
  190.0 150.5 all-gather.10
  342.0 22.8 all-gather.12
  367.0 726.7 reduce-scatter.5
  1096.0 725.6 reduce-scatter.7
  1861.0 385.4 all-gather.14
  2248.1 385.4 all-gather.16
  2635.9 26.9 reduce-scatter.11
  2697.0 26.9 reduce-scatter.13
  2759.5 276.5 reduce-scatter.9
where the time goes:
time: 3060 us; the launch traced here: 3050 us
  waiting for transfers between devices  2650 us (87%)
  matrix products  312 us (10%)
  other arithmetic  63.3 us (2%)
    reduce_scatter x1, waiting for transfers between devices, local_step(): pre_sum = lax.psum_scatter(pre_part, 'cy', scatter_dimension=0, tiled=True)  728 us
    reduce_scatter x1, waiting for transfers between devices, local_step(): h_grad = lax.psum_scatter(h_part, 'cy', scatter_dimension=0, tiled=True)  667 us
    all_gather x1, waiting for transfers between devices, local_step(): grad_full = lax.all_gather(pre_grad, 'cy', axis=0, tiled=True)  385 us
    all_gather x1, waiting for transfers between devices, local_step(): hidden_full = lax.all_gather(hidden, 'cy', axis=0, tiled=True)  324 us
    reduce_scatter x1, waiting for transfers between devices, local_step(): lax.psum_scatter(x_part, 'cz', scatter_dimension=0, tiled=True)  252 us
    all_gather x1, waiting for transfers between devices, local_step(): z_full = lax.all_gather(z_grad, 'cz', axis=0, tiled=True)  153 us
    all_gather x1, waiting for transfers between devices, local_step(): x_full = lax.all_gather(x_act, 'cz', axis=0, tiled=True)  89.7 us
    dot_general x1, matrix products, local_step(): lax.dot_general(hidden_full, z_full, CONTRACT_FIRST, preferred_element_ty...  63.2 us
  transfers between devices with their start and end apart: 11, of which 9 were waited for; matrix products, arithmetic and copies ran while one was open for 11% of the time, Pallas kernels for 0%

commit v1 on v0

v1 whole, which is shorter than its diff:
```python
import functools
import math
import jax
import jax.numpy as jnp
from jax import lax
from jax.experimental import pallas as pl
from jax.experimental.pallas import tpu as pltpu
from jax.sharding import PartitionSpec as P

GELU_COEF = 0.044715
SQRT_TWO_PI = math.sqrt(2.0 / math.pi)
LAST = (((1,), (1,)), ((), ()))
FIRST = (((0,), (0,)), ((), ()))
SWAP = [(0, 1), (1, 0)]
F32 = jnp.float32
BF16 = jnp.bfloat16


def dot(a, b, dims=(((1,), (0,)), ((), ()))):
    return lax.dot_general(a, b, dims, preferred_element_type=F32)


def hidden_kernel(xo, xx, go, gx, wuo, wux, doa, dob, dxa, dxb, *rest):
    h_ref, dc_ref = rest[-2:]
    q = doa.shape[1]
    pre = dot(xo[...], wuo[...]) + dot(xx[...], wux[...])
    c = pre.astype(BF16).astype(F32)
    t = jnp.tanh(SQRT_TWO_PI * (c + GELU_COEF * c * c * c))
    h_ref[...] = (0.5 * c * (1.0 + t)).astype(BF16)
    slope = 0.5 * (1.0 + t) + 0.5 * c * (1.0 - t * t) * SQRT_TWO_PI * (1.0 + 3.0 * GELU_COEF * c * c)
    dh = dot(go[:, :q], doa[...], LAST) + dot(go[:, q:], dob[...], LAST)
    dh += dot(gx[:, :q], dxa[...], LAST) + dot(gx[:, q:], dxb[...], LAST)
    dc_ref[...] = (dh * slope).astype(BF16)


def hidden_call(rows, own, cross, half, wuo, wux, downs, after, bm=512, bn=512):
    (xo, xo_row), (go, go_row) = own
    (xx, xx_row), (gx, gx_row) = cross
    width = wuo.shape[1]
    depth = xo.shape[1]
    bm = min(bm, rows)

    def row_spec(row0):
        return pl.BlockSpec((bm, depth), lambda n, m, r=row0 // bm: (m + r, 0))

    up_spec = pl.BlockSpec((depth, bn), lambda n, m: (0, n))
    shift = half * (width // bn)
    down_spec = pl.BlockSpec((bn, downs[0].shape[1]), lambda n, m: (n + shift, 0))
    out_spec = pl.BlockSpec((bm, bn), lambda n, m: (m, n))
    out = jax.ShapeDtypeStruct((rows, width), BF16)
    extra = [pl.BlockSpec(memory_space=pl.ANY)] * len(after)
    return pl.pallas_call(
        hidden_kernel,
        grid=(width // bn, rows // bm),
        in_specs=[row_spec(xo_row), row_spec(xx_row), row_spec(go_row), row_spec(gx_row), up_spec, up_spec] + [down_spec] * 4 + extra,
        out_specs=[out_spec, out_spec],
        out_shape=[out, out],
        compiler_params=pltpu.CompilerParams(vmem_limit_bytes=56 * 2**20, dimension_semantics=("arbitrary", "arbitrary")),
        cost_estimate=pl.CostEstimate(flops=8 * rows * depth * width, bytes_accessed=4 * rows * depth * 2 + 4 * depth * width * 2, transcendentals=rows * width),
    )(xo, xx, go, gx, wuo, wux, *downs, *after)


def solution(mesh):
    row_spec = P(("dp", "cx", "cz"), "cy")
    up_spec = P("cy", ("cz", "cx"))
    down_spec = P("cz", ("cy", "cx"))
    up_out = P(("dp", "cy"), ("cz", "cx"))
    down_out = P(("dp", "cz"), ("cy", "cx"))

    def swap(v, axis):
        return lax.ppermute(v, axis, SWAP)

    def body(x, w_up, w_down, z):
        first = lax.axis_index("cx") == 0
        nt = x.shape[0]
        h = nt // 2
        q = w_down.shape[1]
        ff = w_up.shape[1]
        g = jnp.where(first, z, jnp.concatenate([z[:, q:], z[:, :q]], axis=1))
        wd = jnp.where(first, w_down, jnp.concatenate([w_down[ff:], w_down[:ff]], axis=0))

        x1, x2, g1, g2 = x[:h], x[h:], g[:h], g[h:]
        xy2 = swap(x2, "cz")
        gy2 = swap(g2, "cz")
        xy1 = swap(x1, "cz")
        gy1 = swap(g1, "cz")
        wu_x = swap(w_up, "cy")
        wd_x = swap(wd, "cy")
        xx1 = swap(x1, "cy")
        gx1 = swap(g1, "cy")
        xb2 = swap(xy2, "cy")
        gb2 = swap(gy2, "cy")
        xx2 = swap(x2, "cy")
        gx2 = swap(g2, "cy")
        wu_p = swap(w_up, "cx")
        wd_p = swap(jnp.concatenate([wd[ff:], wd[:ff]], axis=0), "cx")
        wux_p = swap(wu_x, "cx")
        wdx_p = swap(jnp.concatenate([wd_x[ff:], wd_x[:ff]], axis=0), "cx")
        xa1 = swap(xx1, "cz")
        ga1 = swap(gx1, "cz")

        downs = (wd, wd_p, wd_x, wdx_p)

        def unit(rows, own, cross, after):
            h0, c0 = hidden_call(rows, own, cross, 0, w_up, wu_x, downs, after)
            h1, c1 = hidden_call(rows, own, cross, 1, wu_p, wux_p, downs, (c0,))
            return (h0, h1), (c0, c1)

        def dx_part(dc):
            return dot(dc[0], w_up, LAST) + dot(dc[1], wu_p, LAST)

        h_o1, c_o1 = unit(h, ((x, 0), (g, 0)), ((xx1, 0), (gx1, 0)), ())
        h_a, c_a = unit(h, ((xy1, 0), (gy1, 0)), ((xa1, 0), (ga1, 0)), (c_o1[1],))
        dx_a = swap(dx_part(c_a), "cz")
        h_b, c_b = unit(h, ((xy2, 0), (gy2, 0)), ((xb2, 0), (gb2, 0)), (c_a[1],))
        dx_b = swap(dx_part(c_b), "cz")
        h_o2, c_o2 = unit(h, ((x, h), (g, h)), ((xx2, 0), (gx2, 0)), (c_b[1],))
        dx1 = (dx_part(c_o1) + dx_a).astype(BF16)
        dx2 = (dx_part(c_o2) + dx_b).astype(BF16)
        x_grad = jnp.concatenate([dx1, dx2], axis=0)

        xs = (x1, xy1, xy2, x2)
        gs = (g1, gy1, gy2, g2)
        hs = (h_o1, h_a, h_b, h_o2)
        cs = (c_o1, c_a, c_b, c_o2)

        def total(parts):
            return functools.reduce(lambda a, b: a + b, parts)

        up_send = total([dot(v, c[1], FIRST) for v, c in zip(xs, cs)])
        up_recv = swap(up_send, "cx")
        down_recv = []
        for half in range(2):
            send = total([dot(v[1 - half], w[:, q:], FIRST) for v, w in zip(hs, gs)])
            down_recv.append(swap(send, "cx"))
        up_grad = (total([dot(v, c[0], FIRST) for v, c in zip(xs, cs)]) + up_recv).astype(BF16)
        downs_out = [(total([dot(v[half], w[:, :q], FIRST) for v, w in zip(hs, gs)]) + down_recv[half]).astype(BF16) for half in range(2)]
        down_grad = jnp.where(first, jnp.concatenate(downs_out, axis=0), jnp.concatenate(downs_out[::-1], axis=0))
        return (x_grad, up_grad, down_grad)

    return jax.shard_map(body, mesh=mesh, in_specs=(row_spec, up_spec, down_spec, row_spec), out_specs=(row_spec, up_out, down_out), check_vma=False)
```

time: 3060 us -> 1540 us (0.50)
  waiting for transfers between devices: 2650 us -> 773 us
  Pallas kernels: 0 us -> 307 us
    reduce_scatter x5 -> x0, waiting for transfers between devices: 1650 us -> none  [the longest x1 728 us: local_step(): pre_sum = lax.psum_scatter(pre_part, 'cy', scatter_dimension=0, tiled=True)]
    all_gather x6 -> x0, waiting for transfers between devices: 1000 us -> none  [the longest x1 385 us: local_step(): grad_full = lax.all_gather(pre_grad, 'cy', axis=0, tiled=True)]
    ppermute x0 -> x23, waiting for transfers between devices: none -> 773 us  [swap(): return lax.ppermute(v, axis, SWAP)]
    pallas_call x0 -> x8, Pallas kernels: none -> 307 us  [hidden_call(): pl.pallas_call(hidden_kernel, grid=(width // bn, rows // bm), in_specs=[r...]
    dot_general x5 -> x32, matrix products: 312 us -> 310 us  [dot(): return lax.dot_general(a, b, dims, preferred_element_type=F32)]
  transfers between devices with their start and end apart: 11 -> 23, of which waited for: 9 -> 9; matrix products, arithmetic and copies ran while one was open for 11% -> 22% of each run, Pallas kernels for 0% -> 15%
where the time goes in v1:
time: 1540 us; the launch traced here: 1530 us
  waiting for transfers between devices  773 us (50%)
  matrix products  310 us (20%)
  Pallas kernels  307 us (20%)
  other arithmetic  82.7 us (5%)
  local copies, waits for them, and re-layouts  35 us (2%)
  starting transfers between devices  23.7 us (2%)
    ppermute x23, waiting for transfers between devices, swap(): return lax.ppermute(v, axis, SWAP)  773 us
    dot_general x32, matrix products, dot(): return lax.dot_general(a, b, dims, preferred_element_type=F32)  310 us
    pallas_call x8, Pallas kernels, hidden_call(): pl.pallas_call(hidden_kernel, grid=(width // bn, rows // bm), in_specs=[r...  307 us
  transfers between devices with their start and end apart: 23, of which 9 were waited for; matrix products, arithmetic and copies ran while one was open for 22% of the time, Pallas kernels for 15%

profile of v1, /device:TPU:0, one launch (start us, length us, event | category | flops | bytes accessed | tf_op | source)
XLA Modules:
  0.0 1533.0 jit_solution(14401431244811649583)
XLA Ops:
  0.6 6.0 fusion.44
  6.6 5.5 maximum_select_fusion.1.doa
  12.2 3.3 collective-permute-start.4
  15.5 3.5 fusion.43
  19.0 6.1 pad_maximum_fusion
  30.1 121.9 %collective-permute-done.4.dxa = bf16[4096,768]{1,0:T(8,128)(2,1)} collective-permute-done((bf16[4096,768]{1,0:T(8,128)(2,1)S(1)}, bf16[4096,768]{1,0:T(8,128)(2,1)}, u32[]{:S(2)}, u32[]{:S(2)}) %collective-permute-start.4) | collective-permute-done | bytes 6291488 | tf_op jit(solution)/shard_map/ppermute | solution.py:71
  152.0 3.3 fusion.42
  158.3 4.2 maximum_select_fusion.go
  162.5 3.4 fusion.40
  169.2 5.9 fusion.41
  175.0 179.2 %collective-permute-done.1.gx = bf16[1024,1536]{1,0:T(8,128)(2,1)} collective-permute-done((bf16[1024,1536]{1,0:T(8,128)(2,1)}, bf16[1024,1536]{1,0:T(8,128)(2,1)}, u32[]{:S(2)}, u32[]{:S(2)}) %collective-permute-start.1) | collective-permute-done | bytes 3145760 | tf_op jit(solution)/shard_map/ppermute | solution.py:71
  354.7 64.5 %collective-permute-done.xx = bf16[1024,1536]{1,0:T(8,128)(2,1)S(1)} collective-permute-done((bf16[1024,1536]{1,0:T(8,128)(2,1)}, bf16[1024,1536]{1,0:T(8,128)(2,1)S(1)}, u32[]{:S(2)}, u32[]{:S(2)}) %collective-permute-start) | collective-permute-done | bytes 3145760 | tf_op jit(solution)/shard_map/ppermute | solution.py:71
  423.1 38.4 %shard_map.67 = (bf16[1024,2048]{1,0:T(8,128)(2,1)}, bf16[1024,2048]{1,0:T(8,128)(2,1)}) custom-call(bf16[2048,1536]{1,0:T(8,128)(2,1)} %xo.7, bf16[1024,1536]{1,0:T(8,128)(2,1)} %copy-done.5, bf16[2048,1536]{1,0:T(8,128)(2,1)} %copy-done, bf16[1024,1536]{1,0:T(8,128)(2,1)} %collective-permute-done.1.gx, bf16[1536,2048]{1,0:T(8,128)(2,1)} %wuo.7, ...), custom_call_target="tpu_custom_call" | custom-call | flops 25769803776 | bytes 37748736 | tf_op jit(solution)/shard_map/pallas_call | solution.py:52
  461.5 11.5 fusion.38
  475.1 38.2 %shard_map.68 = (bf16[1024,2048]{1,0:T(8,128)(2,1)}, bf16[1024,2048]{1,0:T(8,128)(2,1)}) custom-call(bf16[2048,1536]{1,0:T(8,128)(2,1)} %xo.7, bf16[1024,1536]{1,0:T(8,128)(2,1)} %copy-done.5, bf16[2048,1536]{1,0:T(8,128)(2,1)} %copy-done, bf16[1024,1536]{1,0:T(8,128)(2,1)} %collective-permute-done.1.gx, bf16[1536,2048]{1,0:T(8,128)(2,1)} %collective-permute-done.6.wuo, ...), custom_call_target="tpu_custom_call" | custom-call | flops 25769803776 | bytes 37748736 | tf_op jit(solution)/shard_map/pallas_call | solution.py:52
  513.6 11.8 fusion.36
  525.5 10.7 fusion.46
  536.1 21.8 %collective-permute-done.8.xo = bf16[1024,1536]{1,0:T(8,128)(2,1)} collective-permute-done((bf16[1024,1536]{1,0:T(8,128)(2,1)}, bf16[1024,1536]{1,0:T(8,128)(2,1)}, u32[]{:S(2)}, u32[]{:S(2)}) %collective-permute-start.8) | collective-permute-done | bytes 3145760 | tf_op jit(solution)/shard_map/ppermute | solution.py:71
  559.7 65.7 %collective-permute-done.17.go = bf16[1024,1536]{1,0:T(8,128)(2,1)} collective-permute-done((bf16[1024,1536]{1,0:T(8,128)(2,1)}, bf16[1024,1536]{1,0:T(8,128)(2,1)}, u32[]{:S(2)}, u32[]{:S(2)}) %collective-permute-start.17) | collective-permute-done | bytes 3145760 | tf_op jit(solution)/shard_map/ppermute | solution.py:71
  627.1 65.7 %collective-permute-done.15.xo = bf16[1024,1536]{1,0:T(8,128)(2,1)} collective-permute-done((bf16[1024,1536]{1,0:T(8,128)(2,1)}, bf16[1024,1536]{1,0:T(8,128)(2,1)}, u32[]{:S(2)}, u32[]{:S(2)}) %collective-permute-start.15) | collective-permute-done | bytes 3145760 | tf_op jit(solution)/shard_map/ppermute | solution.py:71
  694.5 65.7 %collective-permute-done.11.gx = bf16[1024,1536]{1,0:T(8,128)(2,1)} collective-permute-done((bf16[1024,1536]{1,0:T(8,128)(2,1)}, bf16[1024,1536]{1,0:T(8,128)(2,1)}, u32[]{:S(2)}, u32[]{:S(2)}) %collective-permute-start.11) | collective-permute-done | bytes 3145760 | tf_op jit(solution)/shard_map/ppermute | solution.py:71
  761.9 62.6 %collective-permute-done.9.xx = bf16[1024,1536]{1,0:T(8,128)(2,1)} collective-permute-done((bf16[1024,1536]{1,0:T(8,128)(2,1)}, bf16[1024,1536]{1,0:T(8,128)(2,1)}, u32[]{:S(2)}, u32[]{:S(2)}) %collective-permute-start.9) | collective-permute-done | bytes 3145760 | tf_op jit(solution)/shard_map/ppermute | solution.py:71
  824.5 38.1 %shard_map.69 = (bf16[1024,2048]{1,0:T(8,128)(2,1)}, bf16[1024,2048]{1,0:T(8,128)(2,1)}) custom-call(bf16[1024,1536]{1,0:T(8,128)(2,1)} %collective-permute-done.8.xo, bf16[1024,1536]{1,0:T(8,128)(2,1)} %collective-permute-done.9.xx, bf16[1024,1536]{1,0:T(8,128)(2,1)} %collective-permute-done.10.go, bf16[1024,1536]{1,0:T(8,128)(2,1)} %collective-permute-done.11.gx, ...), custom_call_target="tpu_custom_call" | custom-call | flops 25769803776 | bytes 37748736 | tf_op jit(solution)/shard_map/pallas_call | solution.py:52
  862.6 8.4 fusion.31
  871.0 38.4 %shard_map.70 = (bf16[1024,2048]{1,0:T(8,128)(2,1)}, bf16[1024,2048]{1,0:T(8,128)(2,1)}) custom-call(bf16[1024,1536]{1,0:T(8,128)(2,1)} %collective-permute-done.8.xo, bf16[1024,1536]{1,0:T(8,128)(2,1)} %collective-permute-done.9.xx, bf16[1024,1536]{1,0:T(8,128)(2,1)} %collective-permute-done.10.go, bf16[1024,1536]{1,0:T(8,128)(2,1)} %collective-permute-done.11.gx, ...), custom_call_target="tpu_custom_call" | custom-call | flops 25769803776 | bytes 37748736 | tf_op jit(solution)/shard_map/pallas_call | solution.py:52
  909.4 38.1 %shard_map.71 = (bf16[1024,2048]{1,0:T(8,128)(2,1)}, bf16[1024,2048]{1,0:T(8,128)(2,1)}) custom-call(bf16[1024,1536]{1,0:T(8,128)(2,1)} %collective-permute-done.15.xo, bf16[1024,1536]{1,0:T(8,128)(2,1)} %collective-permute-done.16.xx, bf16[1024,1536]{1,0:T(8,128)(2,1)} %collective-permute-done.17.go, bf16[1024,1536]{1,0:T(8,128)(2,1)} %collective-permute-done.18.gx, ...), custom_call_target="tpu_custom_call" | custom-call | flops 25769803776 | bytes 37748736 | tf_op jit(solution)/shard_map/pallas_call | solution.py:52
  947.5 8.4 fusion.14
  955.9 38.3 %shard_map.72 = (bf16[1024,2048]{1,0:T(8,128)(2,1)}, bf16[1024,2048]{1,0:T(8,128)(2,1)}) custom-call(bf16[1024,1536]{1,0:T(8,128)(2,1)} %collective-permute-done.15.xo, bf16[1024,1536]{1,0:T(8,128)(2,1)} %collective-permute-done.16.xx, bf16[1024,1536]{1,0:T(8,128)(2,1)} %collective-permute-done.17.go, bf16[1024,1536]{1,0:T(8,128)(2,1)} %collective-permute-done.18.gx, ...), custom_call_target="tpu_custom_call" | custom-call | flops 25769803776 | bytes 37748736 | tf_op jit(solution)/shard_map/pallas_call | solution.py:52
  994.2 38.7 %shard_map.73 = (bf16[1024,2048]{1,0:T(8,128)(2,1)}, bf16[1024,2048]{1,0:T(8,128)(2,1)}) custom-call(bf16[2048,1536]{1,0:T(8,128)(2,1)} %xo.7, bf16[1024,1536]{1,0:T(8,128)(2,1)} %collective-permute-done.13.xx, bf16[2048,1536]{1,0:T(8,128)(2,1)} %copy-done, bf16[1024,1536]{1,0:T(8,128)(2,1)} %collective-permute-done.14.gx, bf16[1536,2048]{1,0:T(8,128)(2,1)} %wuo.7, ...), custom_call_target="tpu_custom_call" | custom-call | flops 25769803776 | bytes 37748736 | tf_op jit(solution)/shard_map/pallas_call | solution.py:52
  1033.0 11.6 fusion.34
  1044.6 10.6 fusion.49
  1055.2 5.0 fusion.16
  1060.3 38.7 %shard_map.74 = (bf16[1024,2048]{1,0:T(8,128)(2,1)}, bf16[1024,2048]{1,0:T(8,128)(2,1)}) custom-call(bf16[2048,1536]{1,0:T(8,128)(2,1)} %xo.7, bf16[1024,1536]{1,0:T(8,128)(2,1)} %collective-permute-done.13.xx, bf16[2048,1536]{1,0:T(8,128)(2,1)} %copy-done, bf16[1024,1536]{1,0:T(8,128)(2,1)} %collective-permute-done.14.gx, ...), custom_call_target="tpu_custom_call" | custom-call | flops 25769803776 | bytes 37748736 | tf_op jit(solution)/shard_map/pallas_call | solution.py:52
  1099.0 9.0 fusion.8
  1108.0 7.0 fusion.12
  1115.1 8.5 add_add_fusion.1
  1123.6 6.0 fusion.6
  1129.7 7.2 fusion.10
  1136.9 11.2 add_add_fusion
  1148.6 12.8 fusion.55
  1161.4 12.0 fusion.54
  1173.4 20.9 %add_bitcast_fusion = f32[1536,2048]{0,1:T(8,128)} fusion(f32[2048,1536]{1,0:T(8,128)} %fusion.55, f32[2048,1536]{1,0:T(8,128)} %fusion.36, f32[2048,1536]{1,0:T(8,128)} %fusion.54, bf16[1024,2048]{1,0:T(8,128)(2,1)} %get-tuple-element.26, bf16[2048,1536]{1,0:T(8,128)(2,1)} %xo.7), kind=kOutput, calls=%fused_computation.2 | convolution fusion | flops 6451888128 | bytes 57671680 | tf_op jit(solution)/shard_map/dot_general | solution.py:20
  1194.3 10.2 fusion.48
  1204.5 10.8 convolution_add_fusion.1
  1216.8 8.8 fusion.51
  1225.7 10.5 convolution_add_fusion
  1237.0 11.9 fusion.53
  1248.9 10.9 fusion.47
  1259.8 10.8 fusion.50
  1270.7 5.5 fusion.19
  1276.2 5.5 fusion.29
  1281.7 12.1 fusion.52
  1293.9 7.1 fusion.23
  1301.0 7.0 fusion.27
  1308.0 7.0 fusion.21
  1315.0 7.0 fusion.25
  1322.1 11.2 add_convert_fusion.1
  1333.3 12.2 add_convert_fusion
  1345.6 8.6 maximum_select_fusion.2
  1354.2 8.3 add_convert_fusion.3
  1362.5 126.1 %collective-permute-done.19 = f32[1024,1536]{1,0:T(8,128)} collective-permute-done((f32[1024,1536]{1,0:T(8,128)}, f32[1024,1536]{1,0:T(8,128)}, u32[]{:S(2)}, u32[]{:S(2)}) %collective-permute-start.19) | collective-permute-done | bytes 6291488 | tf_op jit(solution)/shard_map/ppermute | solution.py:71
  1488.6 8.2 add_convert_fusion.2
  1499.9 24.3 %fusion = bf16[1536,2048]{0,1:T(8,128)(2,1)} fusion(f32[1536,2048]{0,1:T(8,128)} %collective-permute-done.20, f32[2048,1536]{1,0:T(8,128)} %fusion.34, f32[2048,1536]{1,0:T(8,128)} %fusion.53, f32[2048,1536]{1,0:T(8,128)} %fusion.38, f32[2048,1536]{1,0:T(8,128)} %fusion.52), kind=kLoop, calls=%fused_computation.1 | loop fusion | flops 15728640 | bytes 69206016 | tf_op jit(solution)/shard_map/convert_element_type | solution.py:136
  1524.2 8.6 copy.7
  (128 shorter events, 31.0 us)
Async XLA Ops:
  12.1 6.9 copy-start.3
  12.2 139.8 %collective-permute-start.4 = (bf16[4096,768]{1,0:T(8,128)(2,1)S(1)}, bf16[4096,768]{1,0:T(8,128)(2,1)}, u32[]{:S(2)}, u32[]{:S(2)}) collective-permute-start(bf16[4096,768]{1,0:T(8,128)(2,1)S(1)} %maximum_select_fusion.1.doa), channel_id=1, source_target_pairs={{0,2},{2,0},{1,3},{3,1},{4,6},{6,4},{5,7},{7,5}} | collective-permute-start | bytes 18874376 | tf_op jit(solution)/shard_map/ppermute | solution.py:71
  15.5 11.6 slice-start.6
  19.0 8.1 slice-start.7
  25.1 395.9 %collective-permute-start.3 = (bf16[4096,768]{1,0:T(8,128)(2,1)}, bf16[4096,768]{1,0:T(8,128)(2,1)}, u32[]{:S(2)}, u32[]{:S(2)}) collective-permute-start(bf16[4096,768]{1,0:T(8,128)(2,1)} %pad_maximum_fusion), channel_id=1, source_target_pairs={{0,1},{1,0},{2,3},{3,2},{4,5},{5,4},{6,7},{7,6}} | collective-permute-start | bytes 18874376 | tf_op jit(solution)/shard_map/ppermute | solution.py:71
  25.1 329.1 %collective-permute-start.2 = (bf16[1536,2048]{1,0:T(8,128)(2,1)}, bf16[1536,2048]{1,0:T(8,128)(2,1)}, u32[]{:S(2)}, u32[]{:S(2)}) collective-permute-start(bf16[1536,2048]{1,0:T(8,128)(2,1)} %wuo.7), channel_id=1, source_target_pairs={{0,2},{2,0},{1,3},{3,1},{4,6},{6,4},{5,7},{7,5}} | collective-permute-start | bytes 18874376 | tf_op jit(solution)/shard_map/ppermute | solution.py:71
  158.3 263.0 %collective-permute-start.5 = (bf16[4096,768]{1,0:T(8,128)(2,1)}, bf16[4096,768]{1,0:T(8,128)(2,1)}, u32[]{:S(2)}, u32[]{:S(2)}) collective-permute-start(bf16[4096,768]{1,0:T(8,128)(2,1)} %pad_maximum_fusion.1), channel_id=1, source_target_pairs={{0,1},{1,0},{2,3},{3,2},{4,5},{5,4},{6,7},{7,6}} | collective-permute-start | bytes 18874376 | tf_op jit(solution)/shard_map/ppermute | solution.py:71
  162.5 4.6 copy-start
  167.1 187.1 %collective-permute-start.1 = (bf16[1024,1536]{1,0:T(8,128)(2,1)}, bf16[1024,1536]{1,0:T(8,128)(2,1)}, u32[]{:S(2)}, u32[]{:S(2)}) collective-permute-start(bf16[1024,1536]{1,0:T(8,128)(2,1)} %get-tuple-element.38), channel_id=1, source_target_pairs={{0,2},{2,0},{1,3},{3,1},{4,6},{6,4},{5,7},{7,5}} | collective-permute-start | bytes 9437192 | tf_op jit(solution)/shard_map/ppermute | solution.py:71
  175.0 244.2 %collective-permute-start = (bf16[1024,1536]{1,0:T(8,128)(2,1)}, bf16[1024,1536]{1,0:T(8,128)(2,1)S(1)}, u32[]{:S(2)}, u32[]{:S(2)}) collective-permute-start(bf16[1024,1536]{1,0:T(8,128)(2,1)} %get-tuple-element.40), channel_id=1, source_target_pairs={{0,2},{2,0},{1,3},{3,1},{4,6},{6,4},{5,7},{7,5}} | collective-permute-start | bytes 9437192 | tf_op jit(solution)/shard_map/ppermute | solution.py:71
  354.2 118.9 %collective-permute-start.6 = (bf16[1536,2048]{1,0:T(8,128)(2,1)}, bf16[1536,2048]{1,0:T(8,128)(2,1)}, u32[]{:S(2)}, u32[]{:S(2)}) collective-permute-start(bf16[1536,2048]{1,0:T(8,128)(2,1)} %wuo.7), channel_id=1, source_target_pairs={{0,1},{1,0},{2,3},{3,2},{4,5},{5,4},{6,7},{7,6}} | collective-permute-start | bytes 18874376 | tf_op jit(solution)/shard_map/ppermute | solution.py:71
  354.2 119.1 %collective-permute-start.7 = (bf16[1536,2048]{1,0:T(8,128)(2,1)}, bf16[1536,2048]{1,0:T(8,128)(2,1)}, u32[]{:S(2)}, u32[]{:S(2)}) collective-permute-start(bf16[1536,2048]{1,0:T(8,128)(2,1)} %collective-permute-done.2.wux), channel_id=1, source_target_pairs={{0,1},{1,0},{2,3},{3,2},{4,5},{5,4},{6,7},{7,6}} | collective-permute-start | bytes 18874376 | tf_op jit(solution)/shard_map/ppermute | solution.py:71
  419.2 2.0 copy-start.5
  419.2 94.1 %collective-permute-start.10 = (bf16[1024,1536]{1,0:T(8,128)(2,1)}, bf16[1024,1536]{1,0:T(8,128)(2,1)}, u32[]{:S(2)}, u32[]{:S(2)}) collective-permute-start(bf16[1024,1536]{1,0:T(8,128)(2,1)} %get-tuple-element.38), channel_id=1, source_target_pairs={{0,4},{4,0},{1,5},{5,1},{2,6},{6,2},{3,7},{7,3}} | collective-permute-start | bytes 9437192 | tf_op jit(solution)/shard_map/ppermute | solution.py:71
  421.0 136.9 %collective-permute-start.8 = (bf16[1024,1536]{1,0:T(8,128)(2,1)}, bf16[1024,1536]{1,0:T(8,128)(2,1)}, u32[]{:S(2)}, u32[]{:S(2)}) collective-permute-start(bf16[1024,1536]{1,0:T(8,128)(2,1)} %get-tuple-element.40), channel_id=1, source_target_pairs={{0,4},{4,0},{1,5},{5,1},{2,6},{6,2},{3,7},{7,3}} | collective-permute-start | bytes 9437192 | tf_op jit(solution)/shard_map/ppermute | solution.py:71
  421.3 40.2 %slice-start.10 = ((s8[6291456]{0:T(1024)(128)(4,1)}), s8[4194304]{0:T(1024)(128)(4,1)S(1)}, s32[]{:S(2)}) async-start(s8[6291456]{0:T(1024)(128)(4,1)} %bitcast.60), calls=%async_computation.10 | async-start | bytes 8388608
  421.3 40.2 %slice-start.11 = ((s8[6291456]{0:T(1024)(128)(4,1)}), s8[2097152]{0:T(1024)(128)(4,1)S(1)}, s32[]{:S(2)}) async-start(s8[6291456]{0:T(1024)(128)(4,1)} %bitcast.60), calls=%async_computation.11 | async-start | bytes 4194304
  421.3 204.1 %collective-permute-start.17 = (bf16[1024,1536]{1,0:T(8,128)(2,1)}, bf16[1024,1536]{1,0:T(8,128)(2,1)}, u32[]{:S(2)}, u32[]{:S(2)}) collective-permute-start(bf16[1024,1536]{1,0:T(8,128)(2,1)} %get-tuple-element.39), channel_id=1, source_target_pairs={{0,4},{4,0},{1,5},{5,1},{2,6},{6,2},{3,7},{7,3}} | collective-permute-start | bytes 9437192 | tf_op jit(solution)/shard_map/ppermute | solution.py:71
  473.1 40.6 %slice-start.12 = ((s8[6291456]{0:T(1024)(128)(4,1)}), s8[4194304]{0:T(1024)(128)(4,1)S(1)}, s32[]{:S(2)}) async-start(s8[6291456]{0:T(1024)(128)(4,1)} %bitcast.62), calls=%async_computation.12 | async-start | bytes 8388608
  473.1 40.6 %slice-start.13 = ((s8[6291456]{0:T(1024)(128)(4,1)}), s8[2097152]{0:T(1024)(128)(4,1)S(1)}, s32[]{:S(2)}) async-start(s8[6291456]{0:T(1024)(128)(4,1)} %bitcast.62), calls=%async_computation.13 | async-start | bytes 4194304
  473.1 219.7 %collective-permute-start.15 = (bf16[1024,1536]{1,0:T(8,128)(2,1)}, bf16[1024,1536]{1,0:T(8,128)(2,1)}, u32[]{:S(2)}, u32[]{:S(2)}) collective-permute-start(bf16[1024,1536]{1,0:T(8,128)(2,1)} %get-tuple-element.41), channel_id=1, source_target_pairs={{0,4},{4,0},{1,5},{5,1},{2,6},{6,2},{3,7},{7,3}} | collective-permute-start | bytes 9437192 | tf_op jit(solution)/shard_map/ppermute | solution.py:71
  473.3 286.8 %collective-permute-start.11 = (bf16[1024,1536]{1,0:T(8,128)(2,1)}, bf16[1024,1536]{1,0:T(8,128)(2,1)}, u32[]{:S(2)}, u32[]{:S(2)}) collective-permute-start(bf16[1024,1536]{1,0:T(8,128)(2,1)} %collective-permute-done.1.gx), channel_id=1, source_target_pairs={{0,4},{4,0},{1,5},{5,1},{2,6},{6,2},{3,7},{7,3}} | collective-permute-start | bytes 9437192 | tf_op jit(solution)/shard_map/ppermute | solution.py:71
  513.3 311.1 %collective-permute-start.9 = (bf16[1024,1536]{1,0:T(8,128)(2,1)}, bf16[1024,1536]{1,0:T(8,128)(2,1)}, u32[]{:S(2)}, u32[]{:S(2)}) collective-permute-start(bf16[1024,1536]{1,0:T(8,128)(2,1)} %copy-done.5), channel_id=1, source_target_pairs={{0,4},{4,0},{1,5},{5,1},{2,6},{6,2},{3,7},{7,3}} | collective-permute-start | bytes 9437192 | tf_op jit(solution)/shard_map/ppermute | solution.py:71
  513.6 11.8 copy-start.20
  525.4 337.1 %slice-start = ((s8[6291456]{0:T(1024)(128)(4,1)}), s8[4194304]{0:T(1024)(128)(4,1)S(1)}, s32[]{:S(2)}) async-start(s8[6291456]{0:T(1024)(128)(4,1)} %bitcast.50), calls=%async_computation | async-start | bytes 8388608
  536.1 326.5 %slice-start.1 = ((s8[6291456]{0:T(1024)(128)(4,1)}), s8[2097152]{0:T(1024)(128)(4,1)S(1)}, s32[]{:S(2)}) async-start(s8[6291456]{0:T(1024)(128)(4,1)} %bitcast.50), calls=%async_computation.1 | async-start | bytes 4194304
  557.9 436.2 %collective-permute-start.14 = (bf16[1024,1536]{1,0:T(8,128)(2,1)}, bf16[1024,1536]{1,0:T(8,128)(2,1)}, u32[]{:S(2)}, u32[]{:S(2)}) collective-permute-start(bf16[1024,1536]{1,0:T(8,128)(2,1)} %get-tuple-element.39), channel_id=1, source_target_pairs={{0,2},{2,0},{1,3},{3,1},{4,6},{6,4},{5,7},{7,5}} | collective-permute-start | bytes 9437192 | tf_op jit(solution)/shard_map/ppermute | solution.py:71
  625.4 368.8 %collective-permute-start.13 = (bf16[1024,1536]{1,0:T(8,128)(2,1)}, bf16[1024,1536]{1,0:T(8,128)(2,1)}, u32[]{:S(2)}, u32[]{:S(2)}) collective-permute-start(bf16[1024,1536]{1,0:T(8,128)(2,1)} %get-tuple-element.41), channel_id=1, source_target_pairs={{0,2},{2,0},{1,3},{3,1},{4,6},{6,4},{5,7},{7,5}} | collective-permute-start | bytes 9437192 | tf_op jit(solution)/shard_map/ppermute | solution.py:71
  692.8 216.6 %collective-permute-start.18 = (bf16[1024,1536]{1,0:T(8,128)(2,1)}, bf16[1024,1536]{1,0:T(8,128)(2,1)}, u32[]{:S(2)}, u32[]{:S(2)}) collective-permute-start(bf16[1024,1536]{1,0:T(8,128)(2,1)} %collective-permute-done.17.go), channel_id=1, source_target_pairs={{0,2},{2,0},{1,3},{3,1},{4,6},{6,4},{5,7},{7,5}} | collective-permute-start | bytes 9437192 | tf_op jit(solution)/shard_map/ppermute | solution.py:71
  760.2 149.2 %collective-permute-start.16 = (bf16[1024,1536]{1,0:T(8,128)(2,1)}, bf16[1024,1536]{1,0:T(8,128)(2,1)}, u32[]{:S(2)}, u32[]{:S(2)}) collective-permute-start(bf16[1024,1536]{1,0:T(8,128)(2,1)} %collective-permute-done.15.xo), channel_id=1, source_target_pairs={{0,2},{2,0},{1,3},{3,1},{4,6},{6,4},{5,7},{7,5}} | collective-permute-start | bytes 9437192 | tf_op jit(solution)/shard_map/ppermute | solution.py:71
  955.9 77.0 %slice-start.14 = ((s8[6291456]{0:T(1024)(128)(4,1)}), s8[4194304]{0:T(1024)(128)(4,1)S(1)}, s32[]{:S(2)}) async-start(s8[6291456]{0:T(1024)(128)(4,1)} %bitcast.64), calls=%async_computation.14 | async-start | bytes 8388608
  994.2 38.7 %slice-start.15 = ((s8[6291456]{0:T(1024)(128)(4,1)}), s8[2097152]{0:T(1024)(128)(4,1)S(1)}, s32[]{:S(2)}) async-start(s8[6291456]{0:T(1024)(128)(4,1)} %bitcast.64), calls=%async_computation.15 | async-start | bytes 4194304
  1032.9 11.7 copy-start.21
  1044.6 10.6 copy-start.7
  1098.9 9.1 copy-start.9
  1098.9 16.1 %slice-start.2 = ((s8[6291456]{0:T(1024)(128)(4,1)}), s8[4194304]{0:T(1024)(128)(4,1)S(1)}, s32[]{:S(2)}) async-start(s8[6291456]{0:T(1024)(128)(4,1)} %bitcast.52), calls=%async_computation.2 | async-start | bytes 8388608
  1108.0 7.0 slice-start.3
  1108.0 7.0 copy-start.1
  1123.6 198.5 %collective-permute-start.21 = (f32[2048,768]{1,0:T(8,128)}, f32[2048,768]{1,0:T(8,128)}, u32[]{:S(2)}, u32[]{:S(2)}) collective-permute-start(f32[2048,768]{1,0:T(8,128)} %add_add_fusion.1), channel_id=1, source_target_pairs={{0,1},{1,0},{2,3},{3,2},{4,5},{5,4},{6,7},{7,6}} | collective-permute-start | bytes 18874376 | tf_op jit(solution)/shard_map/ppermute | solution.py:71
  1123.6 6.1 copy-start.11
  1123.6 13.3 slice-start.8
  1129.7 7.3 slice-start.9
  1148.2 13.3 copy-start.18
  1148.2 185.2 %collective-permute-start.22 = (f32[2048,768]{1,0:T(8,128)}, f32[2048,768]{1,0:T(8,128)}, u32[]{:S(2)}, u32[]{:S(2)}) collective-permute-start(f32[2048,768]{1,0:T(8,128)} %add_add_fusion), channel_id=1, source_target_pairs={{0,1},{1,0},{2,3},{3,2},{4,5},{5,4},{6,7},{7,6}} | collective-permute-start | bytes 18874376 | tf_op jit(solution)/shard_map/ppermute | solution.py:71
  1194.3 10.2 copy-start.16
  1194.3 305.6 %collective-permute-start.20 = (f32[1536,2048]{0,1:T(8,128)}, f32[1536,2048]{0,1:T(8,128)}, u32[]{:S(2)}, u32[]{:S(2)}) collective-permute-start(f32[1536,2048]{0,1:T(8,128)} %add_bitcast_fusion), channel_id=1, source_target_pairs={{0,1},{1,0},{2,3},{3,2},{4,5},{5,4},{6,7},{7,6}} | collective-permute-start | bytes 37748744 | tf_op jit(solution)/shard_map/ppermute | solution.py:71
  1204.5 12.3 copy-start.19
  1215.4 10.3 copy-start.17
  1215.4 138.8 %collective-permute-start.12 = (f32[1024,1536]{1,0:T(8,128)}, f32[1024,1536]{1,0:T(8,128)}, u32[]{:S(2)}, u32[]{:S(2)}) collective-permute-start(f32[1024,1536]{1,0:T(8,128)} %convolution_add_fusion.1), channel_id=1, source_target_pairs={{0,4},{4,0},{1,5},{5,1},{2,6},{6,2},{3,7},{7,3}} | collective-permute-start | bytes 18874376 | tf_op jit(solution)/shard_map/ppermute | solution.py:71
  1236.2 12.8 copy-start.15
  1236.2 252.4 %collective-permute-start.19 = (f32[1024,1536]{1,0:T(8,128)}, f32[1024,1536]{1,0:T(8,128)}, u32[]{:S(2)}, u32[]{:S(2)}) collective-permute-start(f32[1024,1536]{1,0:T(8,128)} %convolution_add_fusion), channel_id=1, source_target_pairs={{0,4},{4,0},{1,5},{5,1},{2,6},{6,2},{3,7},{7,3}} | collective-permute-start | bytes 18874376 | tf_op jit(solution)/shard_map/ppermute | solution.py:71
  1248.9 10.9 copy-start.6
  1248.9 21.7 %slice-start.4 = ((s8[6291456]{0:T(1024)(128)(4,1)}), s8[4194304]{0:T(1024)(128)(4,1)S(1)}, s32[]{:S(2)}) async-start(s8[6291456]{0:T(1024)(128)(4,1)} %bitcast.54), calls=%async_computation.4 | async-start | bytes 8388608
  1259.8 10.9 slice-start.5
  1259.8 10.9 copy-start.4
  1270.7 5.5 copy-start.8
  1281.7 12.2 copy-start.13
  1293.9 7.1 copy-start.12
  1301.0 7.0 copy-start.14
  1308.0 7.0 copy-start.10
  1308.0 14.1 slice-start.16
  1315.0 7.1 slice-start.17
  1322.1 11.3 copy-start.2
